TPU v7x, 256 devices: a 2x2x32 block of a 4x8x32 slice. The times are simulated.
256 devices in a mesh: group: 4 (over y, x), blk: 64 (over z, core).
Axes of the slice: x: 2, y: 2, z: 32, core: 2. Of those that a mesh axis runs over, the one named last changes fastest.
The devices are a block of a 4x8x32 slice.
Arguments:
- queries: bfloat16 [8, 256, 2048], P('group', 'blk'), parts along dimension 0, may hold values from -160 to 160
- keys: bfloat16 [8, 81920, 256], P('group', 'blk'), parts along dimension 0, may hold values from -4 to 4
- values: bfloat16 [8, 81920, 256], P('group', 'blk'), parts along dimension 0, may hold values from -6 to 6
- lengths: int32 [8], P('group'), parts along dimension 0, may hold values from 61440 to 81920
- offsets: int32 [8], P('group'), parts along dimension 0, may hold values from 51200 to 81664
Outputs:
- attended: bfloat16 [8, 256, 2048], P('group', 'blk'), parts along dimension 0
There are 4 independent parts, one for each index of `group`. A program takes and returns all parts, laid end to end along the dimension named above; each array names one. Nothing has to cross between parts.
All inputs are finite; a program needn't handle non-finite values.
Results may differ from a plain program's by a relative error of at most 0.0085.
Values may be sent and summed in bfloat16 or wider, within the bound.
A program may use at most 64 MiB of HBM per device.

v0:
```python
import math
import jax
import jax.numpy as jnp
from jax import lax
from jax.sharding import PartitionSpec as P

KV_HEADS = 2
HEAD_DIM = 128
masked_low = -1e30


def shard_partial(query_rows, key_rows, value_rows, query_pos, key_pos, lengths):
    micro_count, rows_count, row_width = query_rows.shape
    heads_count = row_width // HEAD_DIM
    group_size = heads_count // KV_HEADS
    query_split = query_rows.reshape(micro_count, rows_count, KV_HEADS, group_size, HEAD_DIM)
    key_split = key_rows.reshape(micro_count, key_rows.shape[1], KV_HEADS, HEAD_DIM)
    value_split = value_rows.reshape(micro_count, value_rows.shape[1], KV_HEADS, HEAD_DIM)
    scores = jnp.einsum(
        "brkgd,bskd->bkgrs", query_split, key_split, preferred_element_type=jnp.float32
    )
    scores = scores * (1.0 / math.sqrt(HEAD_DIM))
    visible = (key_pos[None, None, :] <= query_pos[:, :, None]) & (
        key_pos[None, None, :] < lengths[:, None, None]
    )
    visible = visible[:, None, None, :, :]
    any_visible = jnp.any(visible, axis=-1)
    row_max = jnp.max(jnp.where(visible, scores, masked_low), axis=-1)
    safe_max = jnp.where(any_visible, row_max, 0.0)
    shifted = jnp.where(visible, scores - safe_max[..., None], 0.0)
    weights = jnp.where(visible, jnp.exp(shifted), 0.0)
    totals = jnp.sum(weights, axis=-1)
    bounded = jnp.maximum(totals, 1.0)
    numerator = jnp.einsum(
        "bkgrs,bskd->bkgrd",
        weights.astype(jnp.bfloat16),
        value_split,
        preferred_element_type=jnp.float32,
    )
    partial_value = (numerator / bounded[..., None]).astype(jnp.bfloat16)
    partial_value = jnp.transpose(partial_value, (0, 3, 1, 2, 4)).reshape(
        micro_count, rows_count, row_width
    )
    logsum = jnp.where(any_visible, safe_max + jnp.log(bounded), masked_low)
    logsum = jnp.transpose(logsum, (0, 3, 1, 2)).reshape(micro_count, rows_count, heads_count)
    return (partial_value, logsum)


def body(queries, keys, values, lengths, offsets):
    micro_count, local_rows, row_width = queries.shape
    local_keys = keys.shape[1]
    heads_count = row_width // HEAD_DIM
    shards = lax.axis_size("blk")
    key_pos = lax.axis_index("blk") * local_keys + jnp.arange(local_keys, dtype=jnp.int32)
    visiting = lax.all_gather(queries, "blk", axis=1, tiled=True)
    rows_count = visiting.shape[1]
    block_rows = math.gcd(rows_count, 64)
    block_count = rows_count // block_rows

    def one_block(block_index):
        block_start = block_index * block_rows
        selected = lax.dynamic_slice_in_dim(visiting, block_start, block_rows, 1)
        query_pos = (
            offsets[:, None] + block_start + jnp.arange(block_rows, dtype=jnp.int32)[None, :]
        )
        return shard_partial(selected, keys, values, query_pos, key_pos, lengths)

    block_parts, block_logs = lax.map(one_block, jnp.arange(block_count, dtype=jnp.int32))
    block_parts = jnp.moveaxis(block_parts, 0, 1).reshape(micro_count, rows_count, row_width)
    block_logs = jnp.moveaxis(block_logs, 0, 1).reshape(micro_count, rows_count, heads_count)
    partials = block_parts
    logsums = block_logs
    partials, logsums = (partials, logsums)
    shaped_parts = partials.reshape(micro_count, shards, local_rows, row_width)
    shaped_logs = logsums.reshape(micro_count, shards, local_rows, heads_count)
    home_parts = lax.all_to_all(shaped_parts, "blk", split_axis=1, concat_axis=1, tiled=True)
    home_logs = lax.all_to_all(shaped_logs, "blk", split_axis=1, concat_axis=1, tiled=True)
    row_peak = jnp.max(home_logs, axis=1, keepdims=True)
    scales = jnp.exp(home_logs - row_peak)
    denominator = jnp.sum(scales, axis=1)
    split_parts = home_parts.reshape(micro_count, shards, local_rows, heads_count, HEAD_DIM)
    weighted = jnp.sum(split_parts * scales[..., None], axis=1)
    merged = weighted / denominator[..., None]
    attended = merged.reshape(micro_count, local_rows, row_width).astype(jnp.bfloat16)
    return attended


def solution(mesh):
    return jax.shard_map(
        body,
        mesh=mesh,
        in_specs=(
            P("group", "blk", None),
            P("group", "blk", None),
            P("group", "blk", None),
            P("group"),
            P("group"),
        ),
        out_specs=P("group", "blk", None),
        check_vma=False,
    )
```

profile of v0, /device:TPU:37, one launch (start us, length us, event | category | flops | bytes accessed | tf_op | source)
XLA Modules:
  0.0 481.0 jit_solution(16185152529671269494)
XLA Ops:
  8.1 3.8 reshape.97
  11.9 2.9 reshape.98
  14.9 139.4 %all-gather.2.cloned.1.call-done = bf16[2,256,2048]{2,0,1:T(2,128)(2,1)} async-done(((bf16[2,4,2048]{2,0,1:T(2,128)(2,1)}), bf16[2,256,2048]{2,0,1:T(2,128)(2,1)}) %all-gather.2.cloned.1.call-update) | async-done | bytes 2097168 | tf_op jit(solution)/shard_map/all_gather | solution.py:55
  154.3 71.4 %while.14 = (s32[]{:T(128)}, bf16[4,2,64,2048]{3,2,1,0:T(8,128)(2,1)}, f32[4,2,64,16]{2,3,1,0:T(8,128)S(1)}, s32[4]{0:T(128)S(1)}, s32[2]{0:T(128)S(1)}, /*index...) while((s32[]{:T(128)}, ...), condition=%wide.wide.region_4.5_spmd.clone, body=%wide.wide.region_0.4_spmd.clone.sunk | while | flops 1377611520 | bytes 88389816 | solution.py:68
  157.6 3.0 fusion.38
  161.0 4.3 fusion.39
  165.5 5.4 %divide_convert_fusion.4 = bf16[2,64,2,8,128]{4,3,1,2,0:T(8,128)(2,1)S(1)} fusion(bf16[2,1280,2,128,1]{3,2,1,0,4:T(2,128)(2,1)S(1)} %bitcast.95, f32[2,2,64,8,1280]{4,3,2,1,0:T(8,128)} %copy-done, f32[2,2,8,64]{2,3,1,0:T(8,128)S(1)} %broadcast_select_fusion.3, pred[2,64,1280]{2,1,0:T(8,128)(4,1)S(1)} %compare_and_fusion.3, ...), kind=kOutput, calls=%fused_computation.15.clone.clone.1 | convolution fusion | flops 684720128 | bytes 12500992 | tf_op jit(solution)/shard_map/while/body/eval_jaxpr/bkgrs,bskd->bkgrd/dot_general | solution.py:34
  175.5 3.0 fusion.38
  178.8 4.3 fusion.39
  183.4 5.4 %divide_convert_fusion.4 = bf16[2,64,2,8,128]{4,3,1,2,0:T(8,128)(2,1)S(1)} fusion(bf16[2,1280,2,128,1]{3,2,1,0,4:T(2,128)(2,1)S(1)} %bitcast.95, f32[2,2,64,8,1280]{4,3,2,1,0:T(8,128)} %copy-done, f32[2,2,8,64]{2,3,1,0:T(8,128)S(1)} %broadcast_select_fusion.3, pred[2,64,1280]{2,1,0:T(8,128)(4,1)S(1)} %compare_and_fusion.3, ...), kind=kOutput, calls=%fused_computation.15.clone.clone.1 | convolution fusion | flops 684720128 | bytes 12500992 | tf_op jit(solution)/shard_map/while/body/eval_jaxpr/bkgrs,bskd->bkgrd/dot_general | solution.py:34
  193.4 3.0 fusion.38
  196.7 4.3 fusion.39
  201.3 5.4 %divide_convert_fusion.4 = bf16[2,64,2,8,128]{4,3,1,2,0:T(8,128)(2,1)S(1)} fusion(bf16[2,1280,2,128,1]{3,2,1,0,4:T(2,128)(2,1)S(1)} %bitcast.95, f32[2,2,64,8,1280]{4,3,2,1,0:T(8,128)} %copy-done, f32[2,2,8,64]{2,3,1,0:T(8,128)S(1)} %broadcast_select_fusion.3, pred[2,64,1280]{2,1,0:T(8,128)(4,1)S(1)} %compare_and_fusion.3, ...), kind=kOutput, calls=%fused_computation.15.clone.clone.1 | convolution fusion | flops 684720128 | bytes 12500992 | tf_op jit(solution)/shard_map/while/body/eval_jaxpr/bkgrs,bskd->bkgrd/dot_general | solution.py:34
  211.2 3.0 fusion.38
  214.5 4.3 fusion.39
  219.1 5.4 %divide_convert_fusion.4 = bf16[2,64,2,8,128]{4,3,1,2,0:T(8,128)(2,1)S(1)} fusion(bf16[2,1280,2,128,1]{3,2,1,0,4:T(2,128)(2,1)S(1)} %bitcast.95, f32[2,2,64,8,1280]{4,3,2,1,0:T(8,128)} %copy-done, f32[2,2,8,64]{2,3,1,0:T(8,128)S(1)} %broadcast_select_fusion.3, pred[2,64,1280]{2,1,0:T(8,128)(4,1)S(1)} %compare_and_fusion.3, ...), kind=kOutput, calls=%fused_computation.15.clone.clone.1 | convolution fusion | flops 684720128 | bytes 12500992 | tf_op jit(solution)/shard_map/while/body/eval_jaxpr/bkgrs,bskd->bkgrd/dot_general | solution.py:34
  226.7 13.8 %all-to-all-start.1 = ((f32[64,1,128]{2,1,0:T(1,128)}), f32[64,1,128]{2,1,0:T(1,128)S(1)}, u32[]{:S(2)}, u32[]{:S(2)}) async-start(f32[64,1,128]{2,1,0:T(1,128)} %reshape.95), calls=%async_computation.1 | async-start | bytes 65536 | tf_op jit(solution)/shard_map/all_to_all | solution.py:77
  240.5 5.1 %copy.53 = bf16[2,4,64,2048]{3,0,2,1:T(2,128)(2,1)} copy(bf16[2,4,64,2048]{3,2,0,1:T(8,128)(2,1)} %bitcast.94) | data formatting | bytes 4194304 | tf_op jit(solution)/shard_map/transpose | solution.py:69
  245.6 16.6 %all-to-all-done.1 = f32[64,1,128]{2,1,0:T(1,128)S(1)} async-done(((f32[64,1,128]{2,1,0:T(1,128)}), f32[64,1,128]{2,1,0:T(1,128)S(1)}, u32[]{:S(2)}, u32[]{:S(2)}) %all-to-all-start.1) | async-done | bytes 32800 | tf_op jit(solution)/shard_map/all_to_all | solution.py:77
  262.2 6.6 %all-to-all-start = ((bf16[2,64,4,2048]{3,0,2,1:T(2,128)(2,1)}), bf16[2,64,4,2048]{3,0,2,1:T(2,128)(2,1)S(1)}, u32[]{:S(2)}, u32[]{:S(2)}) async-start(bf16[2,64,4,2048]{3,0,2,1:T(2,128)(2,1)} %bitcast.93), calls=%async_computation | async-start | bytes 4194304 | tf_op jit(solution)/shard_map/all_to_all | solution.py:76
  270.7 2.6 mul.27
  273.3 5.8 %mul.28 = f32[2,64,4,2048]{3,0,2,1:T(2,128)} reshape(f32[2,64,4,16,128]{4,3,0,2,1:T(8,128)} %mul.27) | data formatting | bytes 8388608 | tf_op jit(solution)/shard_map/mul | solution.py:82
  279.2 189.7 %all-to-all-done = bf16[2,64,4,2048]{3,0,2,1:T(2,128)(2,1)S(1)} async-done(((bf16[2,64,4,2048]{3,0,2,1:T(2,128)(2,1)}), bf16[2,64,4,2048]{3,0,2,1:T(2,128)(2,1)S(1)}, u32[]{:S(2)}, u32[]{:S(2)}) %all-to-all-start) | async-done | bytes 2097184 | tf_op jit(solution)/shard_map/all_to_all | solution.py:76
  468.9 4.5 multiply_reduce_fusion
  (108 shorter events, 22.6 us)
Async XLA Ops:
  6.5 147.7 %copy-start.2 = (s32[2]{0:T(128)S(1)}, s32[2]{0:T(128)}, u32[]{:S(2)}) copy-start(s32[2]{0:T(128)} %param.10) | copy-start | bytes 28
  6.5 147.7 %copy-start.3 = (s32[2]{0:T(128)S(1)}, s32[2]{0:T(128)}, u32[]{:S(2)}) copy-start(s32[2]{0:T(128)} %param.11) | copy-start | bytes 28
  6.6 147.7 %all-gather.2.cloned.1.call-start = ((), (), s32[]{:S(2)}) async-start(), calls=%async_computation.2 | async-start | bytes 2129920 | tf_op jit(solution)/shard_map/all_gather | solution.py:55
  160.6 4.7 copy-start
  161.0 4.5 copy-start.1
  178.5 4.7 copy-start
  178.8 4.5 copy-start.1
  196.3 4.7 copy-start
  196.7 4.5 copy-start.1
  214.2 4.7 copy-start
  214.5 4.5 copy-start.1
  226.7 35.6 %all-to-all-start.1 = ((f32[64,1,128]{2,1,0:T(1,128)}), f32[64,1,128]{2,1,0:T(1,128)S(1)}, u32[]{:S(2)}, u32[]{:S(2)}) async-start(f32[64,1,128]{2,1,0:T(1,128)} %reshape.95), calls=%async_computation.1 | async-start | bytes 65536 | tf_op jit(solution)/shard_map/all_to_all | solution.py:77
  262.2 206.7 %all-to-all-start = ((bf16[2,64,4,2048]{3,0,2,1:T(2,128)(2,1)}), bf16[2,64,4,2048]{3,0,2,1:T(2,128)(2,1)S(1)}, u32[]{:S(2)}, u32[]{:S(2)}) async-start(bf16[2,64,4,2048]{3,0,2,1:T(2,128)(2,1)} %bitcast.93), calls=%async_computation | async-start | bytes 4194304 | tf_op jit(solution)/shard_map/all_to_all | solution.py:76
Sparse Core Ops, SparseCore 0:
  9.2 145.0 all-gather.1
where the time goes:
time: 482 us; the launch traced here: 481 us
  waiting for transfers between devices  346 us (72%)
  local copies, waits for them, and re-layouts  38.7 us (8%)
  matrix products  33.6 us (7%)
  other arithmetic  26 us (5%)
  starting transfers between devices  20.4 us (4%)
  between operations  13.5 us (3%)
    all_to_all x1, waiting for transfers between devices, body(): lax.all_to_all(shaped_parts, 'blk', split_axis=1, concat_axis=1, tiled=True)  190 us
    all_gather x1, waiting for transfers between devices, body(): visiting = lax.all_gather(queries, 'blk', axis=1, tiled=True)  139 us
    dot_general x4, matrix products, shard_partial(): jnp.einsum('bkgrs,bskd->bkgrd', weights.astype(jnp.bfloat16), value_split...  21.7 us
    reduce_sum x4, other arithmetic, shard_partial(): totals = jnp.sum(weights, axis=-1)  17.2 us
    all_to_all x1, waiting for transfers between devices, body(): lax.all_to_all(shaped_logs, 'blk', split_axis=1, concat_axis=1, tiled=True)  16.6 us
    all_to_all x1, starting transfers between devices, body(): lax.all_to_all(shaped_logs, 'blk', split_axis=1, concat_axis=1, tiled=True)  13.8 us
    dot_general x4, matrix products, shard_partial(): jnp.einsum('brkgd,bskd->bkgrs', query_split, key_split, preferred_element...  11.8 us
  transfers between devices with their start and end apart: 3, of which 3 were waited for; matrix products, arithmetic and copies ran while one was open for 5% of the time, Pallas kernels for 0%

commit v1 on v0

--- a/solution.py
+++ b/solution.py
@@ -52,7 +52,9 @@
     heads_count = row_width // HEAD_DIM
     shards = lax.axis_size("blk")
     key_pos = lax.axis_index("blk") * local_keys + jnp.arange(local_keys, dtype=jnp.int32)
-    visiting = lax.all_gather(queries, "blk", axis=1, tiled=True)
+    visiting = jnp.concatenate(
+        lax.all_to_all(jnp.stack([queries] * lax.axis_size("blk")), "blk", 0, 0), axis=1
+    )
     rows_count = visiting.shape[1]
     block_rows = math.gcd(rows_count, 64)
     block_count = rows_count // block_rows

time: 482 us -> 553 us (1.15)
  waiting for transfers between devices: 346 us -> 398 us
  starting transfers between devices: 20.4 us -> 48.2 us
  between operations: 13.5 us -> 0.15 us
    all_to_all x0 -> x1, waiting for transfers between devices: none -> 193 us  [body(): lax.all_to_all(jnp.stack([queries] * lax.axis_size('blk')), 'blk', 0, 0)]
    all_gather x1 -> x0, waiting for transfers between devices: 139 us -> none  [body(): visiting = lax.all_gather(queries, 'blk', axis=1, tiled=True)]
    all_to_all x0 -> x1, starting transfers between devices: none -> 34.4 us  [body(): lax.all_to_all(jnp.stack([queries] * lax.axis_size('blk')), 'blk', 0, 0)]
    all_to_all x1, starting transfers between devices: 13.8 us -> 7.8 us  [body(): lax.all_to_all(shaped_logs, 'blk', split_axis=1, concat_axis=1, tiled=True)]
  transfers between devices with their start and end apart: 3 -> 3, of which waited for: 3 -> 3; matrix products, arithmetic and copies ran while one was open for 5% -> 4% of each run, Pallas kernels for 0% -> 0%
where the time goes in v1:
time: 553 us; the launch traced here: 551 us
  waiting for transfers between devices  398 us (72%)
  starting transfers between devices  48.2 us (9%)
  local copies, waits for them, and re-layouts  41.7 us (8%)
  matrix products  33.5 us (6%)
  other arithmetic  26 us (5%)
    all_to_all x1, waiting for transfers between devices, body(): lax.all_to_all(jnp.stack([queries] * lax.axis_size('blk')), 'blk', 0, 0)  193 us
    all_to_all x1, waiting for transfers between devices, body(): lax.all_to_all(shaped_parts, 'blk', split_axis=1, concat_axis=1, tiled=True)  187 us
    all_to_all x1, starting transfers between devices, body(): lax.all_to_all(jnp.stack([queries] * lax.axis_size('blk')), 'blk', 0, 0)  34.4 us
    dot_general x4, matrix products, shard_partial(): jnp.einsum('bkgrs,bskd->bkgrd', weights.astype(jnp.bfloat16), value_split...  21.7 us
    all_to_all x1, waiting for transfers between devices, body(): lax.all_to_all(shaped_logs, 'blk', split_axis=1, concat_axis=1, tiled=True)  17.5 us
    reduce_sum x4, other arithmetic, shard_partial(): totals = jnp.sum(weights, axis=-1)  17.2 us
    dot_general x4, matrix products, shard_partial(): jnp.einsum('brkgd,bskd->bkgrs', query_split, key_split, preferred_element...  11.8 us
  transfers between devices with their start and end apart: 3, of which 3 were waited for; matrix products, arithmetic and copies ran while one was open for 4% of the time, Pallas kernels for 0%

profile of v1, /device:TPU:37, one launch (start us, length us, event | category | flops | bytes accessed | tf_op | source)
XLA Modules:
  0.0 550.8 jit_solution(17782790158396431401)
XLA Ops:
  0.0 3.3 stack.2
  3.3 34.4 %all-to-all-start = ((bf16[64,2,4,2048]{3,2,1,0:T(4,128)(2,1)}), bf16[64,2,4,2048]{3,2,1,0:T(4,128)(2,1)S(1)}, u32[]{:S(2)}, u32[]{:S(2)}) async-start(bf16[64,2,4,2048]{3,2,1,0:T(4,128)(2,1)} %stack.2), calls=%async_computation | async-start | bytes 4194304 | tf_op jit(solution)/shard_map/all_to_all | solution.py:56
  41.9 193.1 %all-to-all-done = bf16[64,2,4,2048]{3,2,1,0:T(4,128)(2,1)S(1)} async-done(((bf16[64,2,4,2048]{3,2,1,0:T(4,128)(2,1)}), bf16[64,2,4,2048]{3,2,1,0:T(4,128)(2,1)S(1)}, u32[]{:S(2)}, u32[]{:S(2)}) %all-to-all-start) | async-done | bytes 2097184 | tf_op jit(solution)/shard_map/all_to_all | solution.py:56
  235.0 3.5 copy.61
  238.4 71.9 %while.14 = (s32[]{:T(128)}, bf16[4,2,64,2048]{3,2,1,0:T(8,128)(2,1)}, f32[4,2,64,16]{2,3,1,0:T(8,128)S(1)}, s32[4]{0:T(128)S(1)}, s32[2]{0:T(128)S(1)}, /*index...) while((s32[]{:T(128)}, ...), condition=%wide.wide.region_4.5_spmd.clone, body=%wide.wide.region_0.4_spmd.clone.sunk | while | flops 1377611520 | bytes 88389816 | solution.py:70
  241.9 3.0 fusion.38
  245.3 4.3 fusion.39
  249.8 5.4 divide_convert_fusion.4
  259.9 3.0 fusion.38
  263.2 4.3 fusion.39
  267.8 5.4 divide_convert_fusion.4
  277.9 3.0 fusion.38
  281.2 4.3 fusion.39
  285.8 5.4 divide_convert_fusion.4
  295.8 3.0 fusion.38
  299.2 4.3 fusion.39
  303.7 5.4 divide_convert_fusion.4
  311.3 7.8 %all-to-all-start.2 = ((f32[64,1,128]{2,1,0:T(1,128)}), f32[64,1,128]{2,1,0:T(1,128)S(1)}, u32[]{:S(2)}, u32[]{:S(2)}) async-start(f32[64,1,128]{2,1,0:T(1,128)} %reshape.105), calls=%async_computation.2 | async-start | bytes 65536 | tf_op jit(solution)/shard_map/all_to_all | solution.py:79
  319.1 5.1 copy.63
  324.3 17.5 %all-to-all-done.2 = f32[64,1,128]{2,1,0:T(1,128)S(1)} async-done(((f32[64,1,128]{2,1,0:T(1,128)}), f32[64,1,128]{2,1,0:T(1,128)S(1)}, u32[]{:S(2)}, u32[]{:S(2)}) %all-to-all-start.2) | async-done | bytes 32800 | tf_op jit(solution)/shard_map/all_to_all | solution.py:79
  341.8 6.0 %all-to-all-start.1 = ((bf16[2,64,4,2048]{3,0,2,1:T(2,128)(2,1)}), bf16[2,64,4,2048]{3,0,2,1:T(2,128)(2,1)S(1)}, u32[]{:S(2)}, u32[]{:S(2)}) async-start(bf16[2,64,4,2048]{3,0,2,1:T(2,128)(2,1)} %bitcast.96), calls=%async_computation.1 | async-start | bytes 4194304 | tf_op jit(solution)/shard_map/all_to_all | solution.py:78
  352.3 5.8 %mul.28 = f32[2,64,4,2048]{3,0,2,1:T(2,128)} reshape(f32[2,64,4,16,128]{4,3,0,2,1:T(8,128)} %mul.27) | data formatting | bytes 8388608 | tf_op jit(solution)/shard_map/mul | solution.py:84
  358.2 187.4 %all-to-all-done.1 = bf16[2,64,4,2048]{3,0,2,1:T(2,128)(2,1)S(1)} async-done(((bf16[2,64,4,2048]{3,0,2,1:T(2,128)(2,1)}), bf16[2,64,4,2048]{3,0,2,1:T(2,128)(2,1)S(1)}, u32[]{:S(2)}, u32[]{:S(2)}) %all-to-all-start.1) | async-done | bytes 2097184 | tf_op jit(solution)/shard_map/all_to_all | solution.py:78
  545.6 4.5 multiply_reduce_fusion
  (110 shorter events, 28.2 us)
Async XLA Ops:
  0.0 37.6 %copy-start.1 = (bf16[2,1280,256]{2,1,0:T(8,128)(2,1)S(1)}, bf16[2,1280,256]{2,1,0:T(8,128)(2,1)}, u32[]{:S(2)}) copy-start(bf16[2,1280,256]{2,1,0:T(8,128)(2,1)} %param.9) | copy-start | bytes 3932164
  3.3 231.7 %all-to-all-start = ((bf16[64,2,4,2048]{3,2,1,0:T(4,128)(2,1)}), bf16[64,2,4,2048]{3,2,1,0:T(4,128)(2,1)S(1)}, u32[]{:S(2)}, u32[]{:S(2)}) async-start(bf16[64,2,4,2048]{3,2,1,0:T(4,128)(2,1)} %stack.2), calls=%async_computation | async-start | bytes 4194304 | tf_op jit(solution)/shard_map/all_to_all | solution.py:56
  37.7 200.8 %copy-start.3 = (s32[2]{0:T(128)S(1)}, s32[2]{0:T(128)}, u32[]{:S(2)}) copy-start(s32[2]{0:T(128)} %param.10) | copy-start | bytes 28
  37.7 200.8 %copy-start.4 = (s32[2]{0:T(128)S(1)}, s32[2]{0:T(128)}, u32[]{:S(2)}) copy-start(s32[2]{0:T(128)} %param.11) | copy-start | bytes 28
  244.9 4.7 copy-start
  245.2 4.5 copy-start.2
  262.9 4.7 copy-start
  263.2 4.5 copy-start.2
  280.9 4.7 copy-start
  281.2 4.5 copy-start.2
  298.8 4.7 copy-start
  299.2 4.5 copy-start.2
  311.3 30.5 %all-to-all-start.2 = ((f32[64,1,128]{2,1,0:T(1,128)}), f32[64,1,128]{2,1,0:T(1,128)S(1)}, u32[]{:S(2)}, u32[]{:S(2)}) async-start(f32[64,1,128]{2,1,0:T(1,128)} %reshape.105), calls=%async_computation.2 | async-start | bytes 65536 | tf_op jit(solution)/shard_map/all_to_all | solution.py:79
  341.8 203.8 %all-to-all-start.1 = ((bf16[2,64,4,2048]{3,0,2,1:T(2,128)(2,1)}), bf16[2,64,4,2048]{3,0,2,1:T(2,128)(2,1)S(1)}, u32[]{:S(2)}, u32[]{:S(2)}) async-start(bf16[2,64,4,2048]{3,0,2,1:T(2,128)(2,1)} %bitcast.96), calls=%async_computation.1 | async-start | bytes 4194304 | tf_op jit(solution)/shard_map/all_to_all | solution.py:78
